TPU v7x, 32 devices: a whole 2x2x4 slice. The times are simulated.
32 devices in a mesh: tp: 4 (over z), dp: 8 (over y, x, core).
Axes of the slice: x: 2, y: 2, z: 4, core: 2. Of those that a mesh axis runs over, the one named last changes fastest.
Arguments:
- tokens: int32 [8, 2048], P('dp')
- cotangent: bfloat16 [8, 2048, 1024], P('dp')
- emb_table: bfloat16 [30592, 1024], P('tp')
- w_qkv: bfloat16 [1024, 3072], P(None, 'tp')
- b_qkv: bfloat16 [16, 192], P('tp')
- w_out: bfloat16 [1024, 1024], P('tp')
- b_out: bfloat16 [1024], replicated
- ln1_gain: bfloat16 [1024], replicated
- ln1_bias: bfloat16 [1024], replicated
- w_gate: bfloat16 [1024, 4096], P(None, 'tp')
- b_gate: bfloat16 [4096], P('tp')
- w_lin: bfloat16 [1024, 4096], P(None, 'tp')
- b_lin: bfloat16 [4096], P('tp')
- w_down: bfloat16 [4096, 1024], P('tp')
- b_down: bfloat16 [1024], replicated
- ln2_gain: bfloat16 [1024], replicated
Outputs:
- output 1: float32 [30592, 1024], P('tp')
- output 2: float32 [1024, 3072], P(None, 'tp')
- output 3: float32 [16, 192], P('tp')
- output 4: float32 [1024, 1024], P('tp')
- output 5: float32 [1024], replicated
- output 6: float32 [1024], replicated
- output 7: float32 [1024], replicated
- output 8: float32 [1024, 4096], P(None, 'tp')
- output 9: float32 [4096], P('tp')
- output 10: float32 [1024, 4096], P(None, 'tp')
- output 11: float32 [4096], P('tp')
- output 12: float32 [4096, 1024], P('tp')
- output 13: float32 [1024], replicated
- output 14: float32 [1024], replicated
All inputs are finite; a program needn't handle non-finite values.
Results may differ from a plain program's by a relative error of at most 0.0152302.
Values sent between devices are 32-bit elements.
A program may use at most 1 GiB of HBM per device.

v0:
```python
import jax
import jax.numpy as jnp
from jax import lax
from jax.sharding import PartitionSpec as P

ALPHA = 140.0 ** 0.5
EPS = 1e-5
SHRINK = 0.1
ROPE_BASE = 10000.0
WEIGHT_SPECS = (P(None, 'tp'), P('tp', None), P('tp', None), P(), P(), P(), P(None, 'tp'), P('tp'), P(None, 'tp'), P('tp'), P('tp', None), P(), P())


def norm_scaled(values, gain):
    mean_val = jnp.mean(values, axis=-1, keepdims=True)
    centered = values - mean_val
    variance = jnp.mean(centered * centered, axis=-1, keepdims=True)
    return centered * lax.rsqrt(variance + EPS) * gain


def geglu(gate_pre, lin_pre):
    return jax.nn.gelu(gate_pre, approximate=False) * lin_pre


def rope_tables(seq_len, head_dim):
    half_dim = head_dim // 2
    inv_freq = ROPE_BASE ** (-2.0 * jnp.arange(half_dim, dtype=jnp.float32) / head_dim)
    angles = jnp.arange(seq_len, dtype=jnp.float32)[:, None] * inv_freq[None, :]
    return jnp.cos(angles)[:, None, :], jnp.sin(angles)[:, None, :]


def apply_rope(values, cos_tab, sin_tab):
    half_dim = values.shape[-1] // 2
    first_half = values[..., :half_dim]
    second_half = values[..., half_dim:]
    return jnp.concatenate([first_half * cos_tab - second_half * sin_tab, second_half * cos_tab + first_half * sin_tab], axis=-1)


def local_layer(embedded, cotangent, weights):
    (w_qkv, b_qkv, w_out, b_out, ln1_gain, ln1_bias, w_gate, b_gate, w_lin, b_lin, w_down, b_down, ln2_gain) = weights
    batch_loc, seq_len = embedded.shape[0], embedded.shape[1]
    heads_loc = b_qkv.shape[0]
    head_dim = b_qkv.shape[1] // 3
    emb_bf = embedded.astype(jnp.bfloat16)
    qkv_pre = jnp.einsum('bsd,de->bse', emb_bf, w_qkv, preferred_element_type=jnp.float32) + b_qkv.reshape(-1).astype(jnp.float32)
    qkv_all = qkv_pre.astype(jnp.bfloat16).reshape(batch_loc, seq_len, heads_loc, 3, head_dim)
    cos_tab, sin_tab = rope_tables(seq_len, head_dim)
    queries = apply_rope(qkv_all[:, :, :, 0].astype(jnp.float32), cos_tab, sin_tab).astype(jnp.bfloat16)
    keys_rot = apply_rope(qkv_all[:, :, :, 1].astype(jnp.float32), cos_tab, sin_tab).astype(jnp.bfloat16)
    values = qkv_all[:, :, :, 2]
    attn_scale = head_dim ** -0.5
    causal = jnp.arange(seq_len)[:, None] >= jnp.arange(seq_len)[None, :]
    scores = jnp.einsum('bqhd,bkhd->bhqk', queries, keys_rot, preferred_element_type=jnp.float32) * attn_scale
    attn_probs = jax.nn.softmax(jnp.where(causal, scores, -1e30), axis=-1).astype(jnp.bfloat16)
    context = jnp.einsum('bhqk,bkhd->bqhd', attn_probs, values, preferred_element_type=jnp.float32).astype(jnp.bfloat16).reshape(batch_loc, seq_len, heads_loc * head_dim)
    attn_part = jnp.einsum('bse,ed->bsd', context, w_out, preferred_element_type=jnp.float32)
    attn_out = lax.psum(attn_part, 'tp') + b_out.astype(jnp.float32)
    normed_one, norm_one_pull = jax.vjp(norm_scaled, ALPHA * embedded + attn_out, ln1_gain.astype(jnp.float32))
    hidden = (normed_one + ln1_bias.astype(jnp.float32)).astype(jnp.bfloat16)
    gate_pre = jnp.einsum('bsd,df->bsf', hidden, w_gate, preferred_element_type=jnp.float32) + b_gate.astype(jnp.float32)
    lin_pre = jnp.einsum('bsd,df->bsf', hidden, w_lin, preferred_element_type=jnp.float32) + b_lin.astype(jnp.float32)
    inner_val, act_pull = jax.vjp(geglu, gate_pre, lin_pre)
    inner_act = inner_val.astype(jnp.bfloat16)
    ffn_part = jnp.einsum('bsf,fd->bsd', inner_act, w_down, preferred_element_type=jnp.float32)
    ffn_out = lax.psum(ffn_part, 'tp') + b_down.astype(jnp.float32)
    norm_two_pull = jax.vjp(norm_scaled, ALPHA * hidden.astype(jnp.float32) + ffn_out, ln2_gain.astype(jnp.float32))[1]

    d_resid_two, d_ln2_gain = norm_two_pull(cotangent.astype(jnp.float32))
    d_b_down = jnp.sum(d_resid_two, axis=(0, 1))
    d_ffn_bf = d_resid_two.astype(jnp.bfloat16)
    d_w_down = jnp.einsum('bsf,bsd->fd', inner_act, d_ffn_bf, preferred_element_type=jnp.float32)
    d_inner = jnp.einsum('bsd,fd->bsf', d_ffn_bf, w_down, preferred_element_type=jnp.float32).astype(jnp.bfloat16)
    d_gate_pre, d_lin_pre = act_pull(d_inner.astype(jnp.float32))
    d_b_gate = jnp.sum(d_gate_pre, axis=(0, 1))
    d_b_lin = jnp.sum(d_lin_pre, axis=(0, 1))
    d_gate_bf = d_gate_pre.astype(jnp.bfloat16)
    d_lin_bf = d_lin_pre.astype(jnp.bfloat16)
    d_w_gate = jnp.einsum('bsd,bsf->df', hidden, d_gate_bf, preferred_element_type=jnp.float32)
    d_w_lin = jnp.einsum('bsd,bsf->df', hidden, d_lin_bf, preferred_element_type=jnp.float32)
    d_hidden_part = jnp.einsum('bsf,df->bsd', d_gate_bf, w_gate, preferred_element_type=jnp.float32) + jnp.einsum('bsf,df->bsd', d_lin_bf, w_lin, preferred_element_type=jnp.float32)
    d_hidden = ALPHA * d_resid_two + lax.psum(d_hidden_part, 'tp')
    d_ln1_bias = jnp.sum(d_hidden, axis=(0, 1))
    d_resid_one, d_ln1_gain = norm_one_pull(d_hidden)
    d_b_out = jnp.sum(d_resid_one, axis=(0, 1))
    d_attn_bf = d_resid_one.astype(jnp.bfloat16)
    d_w_out = jnp.einsum('bse,bsd->ed', context, d_attn_bf, preferred_element_type=jnp.float32)
    d_context = jnp.einsum('bsd,ed->bse', d_attn_bf, w_out, preferred_element_type=jnp.float32).astype(jnp.bfloat16).reshape(batch_loc, seq_len, heads_loc, head_dim)
    d_probs = jnp.einsum('bqhd,bkhd->bhqk', d_context, values, preferred_element_type=jnp.float32)
    d_values = jnp.einsum('bhqk,bqhd->bkhd', attn_probs, d_context, preferred_element_type=jnp.float32)
    probs_f32 = attn_probs.astype(jnp.float32)
    d_scores = (probs_f32 * (d_probs - jnp.sum(d_probs * probs_f32, axis=-1, keepdims=True)) * attn_scale).astype(jnp.bfloat16)
    d_queries = apply_rope(jnp.einsum('bhqk,bkhd->bqhd', d_scores, keys_rot, preferred_element_type=jnp.float32), cos_tab, -sin_tab)
    d_keys = apply_rope(jnp.einsum('bhqk,bqhd->bkhd', d_scores, queries, preferred_element_type=jnp.float32), cos_tab, -sin_tab)
    d_qkv = jnp.stack([d_queries, d_keys, d_values], axis=3).reshape(batch_loc, seq_len, -1)
    d_b_qkv = jnp.sum(d_qkv, axis=(0, 1)).reshape(heads_loc, 3 * head_dim)
    d_qkv_bf = d_qkv.astype(jnp.bfloat16)
    d_w_qkv = jnp.einsum('bsd,bse->de', emb_bf, d_qkv_bf, preferred_element_type=jnp.float32)
    d_emb_part = jnp.einsum('bse,de->bsd', d_qkv_bf, w_qkv, preferred_element_type=jnp.float32)
    d_embedded = ALPHA * d_resid_one + lax.psum(d_emb_part, 'tp')
    grads = (d_w_qkv, d_b_qkv, d_w_out, d_b_out, d_ln1_gain, d_ln1_bias, d_w_gate, d_b_gate, d_w_lin, d_b_lin, d_w_down, d_b_down, d_ln2_gain)
    return d_embedded, grads


def solution(mesh):
    in_specs = (P('dp', None), P('dp', None, None), P('tp', None)) + WEIGHT_SPECS
    out_specs = (P('tp', None),) + WEIGHT_SPECS

    def device_step(tokens, cotangent, emb_table, *weights):
        vocab_loc = emb_table.shape[0]
        local_ids = tokens - lax.axis_index('tp') * vocab_loc
        in_shard = (local_ids >= 0) & (local_ids < vocab_loc)
        safe_ids = jnp.where(in_shard, local_ids, 0)
        own_rows = jnp.where(in_shard[:, :, None], jnp.take(emb_table, safe_ids, axis=0), 0.0)
        embedded = lax.psum(own_rows.astype(jnp.float32), 'tp')
        d_embedded, grads = local_layer(embedded, cotangent, weights)
        d_rows = jnp.where(in_shard[:, :, None], SHRINK * d_embedded, 0.0)
        d_table = jax.ops.segment_sum(d_rows.reshape(-1, d_rows.shape[-1]), safe_ids.reshape(-1), num_segments=vocab_loc)
        return lax.psum((d_table,) + grads, 'dp')

    return jax.shard_map(device_step, mesh=mesh, in_specs=in_specs, out_specs=out_specs, check_vma=False)
```

profile of v0, /device:TPU:0, one launch (start us, length us, event | category | flops | bytes accessed | tf_op | source)
XLA Modules:
  0.0 2518.3 jit_solution(6012257155631353138)
XLA Ops:
  8.7 18.4 gather_fusion
  27.1 5.5 fusion.49
  38.7 285.6 %all-reduce.9.cloned.1.call-done = f32[1,2048,1024]{2,1,0:T(8,128)} async-done(((f32[1,2048,1024]{2,1,0:T(8,128)}), f32[1,2048,1024]{2,1,0:T(8,128)}) %all-reduce.9.cloned.1.call-update) | async-done | bytes 8388624 | tf_op jit(solution)/shard_map/psum | solution.py:113
  324.3 7.3 add_convert_fusion.3
  335.5 34.2 %fusion.103 = (f32[4,2048]{1,0:T(4,128)S(1)}, f32[4,2048,2048]{1,2,0:T(8,128)}) fusion(pred[2048,2048]{0,1:T(8,128)(4,1)} %iota_compare_fusion, bf16[2048,4,32]{0,2,1:T(8,128)(2,1)} %get-tuple-element.64, bf16[2048,4,32]{0,2,1:T(8,128)(2,1)} %get-tuple-element.65, bf16[2048,4,32]{0,2,1:T(8,128)(2,1)} %get-tuple-element.59, ...), kind=kOutput, calls=%fused_computation.171 | convolution fusion | flops 2218788864 | bytes 73433088 | tf_op jit(solution)/shard_map/sub | solution.py:53
  369.7 33.3 %divide_convert_fusion = bf16[4,2048,2048]{1,2,0:T(8,128)(2,1)} fusion(f32[4,2048,2048]{1,2,0:T(8,128)} %get-tuple-element.71, f32[4,2048]{1,0:T(4,128)S(1)} %get-tuple-element.70), kind=kLoop, calls=%fused_computation.8 | loop fusion | flops 33554432 | bytes 100696064 | tf_op jit(solution)/shard_map/convert_element_type | solution.py:53
  403.0 16.9 convolution_convert_fusion.1
  425.7 287.7 %all-reduce.11.cloned.1.call-done = f32[1,2048,1024]{2,1,0:T(8,128)} async-done(((f32[1,2048,1024]{2,1,0:T(8,128)}), f32[1,2048,1024]{2,1,0:T(8,128)}) %all-reduce.11.cloned.1.call-update) | async-done | bytes 8388624 | tf_op jit(solution)/shard_map/psum | solution.py:56
  713.4 10.3 fusion.102
  735.6 23.9 multiply_convert_fusion
  761.5 6.6 convolution_bitcast_fusion
  768.8 287.2 %all-reduce.13.cloned.1.call-done = f32[1,2048,1024]{2,1,0:T(8,128)} async-done(((f32[1,2048,1024]{2,1,0:T(8,128)}), f32[1,2048,1024]{2,1,0:T(8,128)}) %all-reduce.13.cloned.1.call-update) | async-done | bytes 8388624 | tf_op jit(solution)/shard_map/psum | solution.py:64
  1056.0 7.4 fusion.100
  1073.1 22.5 fusion.97
  1095.6 7.1 fusion.59
  1102.8 10.9 add_bitcast_fusion
  1113.8 287.8 %all-reduce.15.cloned.1.call-done = f32[1,2048,1024]{2,1,0:T(8,128)} async-done(((f32[1,2048,1024]{2,1,0:T(8,128)}), f32[1,2048,1024]{2,1,0:T(8,128)}) %all-reduce.15.cloned.1.call-update) | async-done | bytes 8388624 | tf_op jit(solution)/shard_map/psum | solution.py:80
  1401.6 11.5 multiply_reduce_fusion
  1421.2 16.2 convolution_bitcast_fusion.3
  1437.4 24.6 fusion.65
  1462.0 63.4 %fusion.56 = f32[1,2048,4,64]{1,3,2,0:T(8,128)} fusion(bf16[4,2048,2048]{1,2,0:T(8,128)(2,1)} %divide_convert_fusion, f32[4,2048,2048]{1,2,0:T(8,128)} %fusion.65, bf16[2048,4,32]{0,2,1:T(8,128)(2,1)S(1)} %copy-done.30, bf16[2048,4,32]{0,2,1:T(8,128)(2,1)S(1)} %copy-done.31), kind=kOutput, calls=%fused_computation.100 | convolution fusion | flops 2267031552 | bytes 103809024 | tf_op jit(solution)/shard_map/bhqk,bkhd->bqhd/dot_general | solution.py:91
  1525.4 64.2 %fusion.57 = f32[1,2048,4,64]{1,3,2,0:T(8,128)} fusion(bf16[4,2048,2048]{1,2,0:T(8,128)(2,1)} %divide_convert_fusion, f32[4,2048,2048]{1,2,0:T(8,128)} %fusion.65, bf16[2048,4,32]{0,2,1:T(8,128)(2,1)S(1)} %copy-done.29, bf16[2048,4,32]{0,2,1:T(8,128)(2,1)S(1)} %copy-done.28), kind=kOutput, calls=%fused_computation.101 | convolution fusion | flops 2267031552 | bytes 103809024 | tf_op jit(solution)/shard_map/bhqk,bqhd->bkhd/dot_general | solution.py:92
  1596.5 5.8 convolution_bitcast_fusion.1
  1602.4 10.1 fusion.38
  1612.6 10.1 fusion.89
  1622.6 10.0 fusion.36
  1635.1 5.2 fusion.44
  1640.3 249.9 %all-reduce.17.cloned.1.call-done = f32[1,2048,1024]{2,1,0:T(8,128)} async-done(((f32[1,2048,1024]{2,1,0:T(8,128)}), f32[1,2048,1024]{2,1,0:T(8,128)}) %all-reduce.17.cloned.1.call-update) | async-done | bytes 8388624 | tf_op jit(solution)/shard_map/psum | solution.py:98
  1890.2 33.6 %scatter_custom_fusion = f32[7648,1024]{1,0:T(8,128)} fusion(s32[2048]{0:T(1024)} %bitcast.139, f32[]{:T(128)} %constant.47.clone.1, f32[1,2048,1024]{2,1,0:T(8,128)} %all-reduce.17.cloned.1.call-done, f32[]{:T(128)} %constant.122.clone.1, f32[1,2048,1024]{2,1,0:T(8,128)} %copy-done.3, f32[2048]{0:T(1024)S(1)} %negate_multiply_fusion.1, ...), kind=kCustom, calls=%fused_computation.19 | custom fusion | flops 12582912 | bytes 48115712 | tf_op jit(solution)/shard_map/scatter-add | solution.py:116
  1932.2 24.9 all-reduce
  1957.1 519.3 %all-reduce.19.cloned.1.call-done = (f32[7648,1024]{1,0:T(8,128)}, f32[1024,768]{1,0:T(8,128)}, f32[256,1024]{1,0:T(8,128)}, f32[1024,1024]{1,0:T(8,128)}, f32[1024,1024]{1,0:T(8,128)}, /*index=5*/f32[1024,1024]{1,0:T(8,128)}) async-done(((f32[7648,1024]{1,0:T(8,128)}, f32[1024,768]{1,0:T(8,128)}, f32[256,1024]{1,0:T(8,128)}, f32[1024,1024]{1,0:T(8,128)}, f32[1024,1024]{1,0:T(8,128)}, ...) | async-done | bytes 48103440 | tf_op jit(solution)/shard_map/psum | solution.py:117
  2476.5 23.1 copy.72
  (184 shorter events, 78.7 us)
Async XLA Ops:
  7.2 728.4 %copy-start = (bf16[1024,1024]{1,0:T(8,128)(2,1)S(1)}, bf16[1024,1024]{1,0:T(8,128)(2,1)}, u32[]{:S(2)}) copy-start(bf16[1024,1024]{1,0:T(8,128)(2,1)} %param.27) | copy-start | bytes 6291460
  7.2 317.1 %all-reduce.9.cloned.1.call-start = ((), (), s32[]{:S(2)}) async-start(), calls=%async_computation | async-start | bytes 16777216 | tf_op jit(solution)/shard_map/psum | solution.py:113
  8.7 18.4 copy-start.34
  32.6 680.8 %all-reduce.11.cloned.1.call-start = ((), (), s32[]{:S(2)}) async-start(), calls=%async_computation.1 | async-start | bytes 16777216 | tf_op jit(solution)/shard_map/psum | solution.py:56
  34.5 299.2 %copy-start.21 = (f32[2048,32]{0,1:T(8,128)}, f32[2048,32]{0,1:T(8,128)S(1)}, u32[]{:S(2)}) copy-start(f32[2048,32]{0,1:T(8,128)S(1)} %get-tuple-element.69) | copy-start | bytes 786436
  335.5 34.2 %copy-start.27 = (bf16[2048,4,32]{0,2,1:T(8,128)(2,1)}, bf16[2048,4,32]{0,2,1:T(8,128)(2,1)S(1)}, u32[]{:S(2)}) copy-start(bf16[2048,4,32]{0,2,1:T(8,128)(2,1)S(1)} %get-tuple-element.58) | copy-start | bytes 1572868
  403.0 17.8 copy-start.25
  425.6 630.4 %all-reduce.13.cloned.1.call-start = ((), (), s32[]{:S(2)}) async-start(), calls=%async_computation.2 | async-start | bytes 16777216 | tf_op jit(solution)/shard_map/psum | solution.py:64
  735.6 23.9 copy-start.53
  735.6 25.9 %copy-start.50 = (bf16[1024,1024]{1,0:T(8,128)(2,1)S(1)}, bf16[1024,1024]{1,0:T(8,128)(2,1)}, u32[]{:S(2)}) copy-start(bf16[1024,1024]{1,0:T(8,128)(2,1)} %param.29) | copy-start | bytes 6291460
  768.1 633.5 %all-reduce.15.cloned.1.call-start = ((), (), s32[]{:S(2)}) async-start(), calls=%async_computation.3 | async-start | bytes 16777216 | tf_op jit(solution)/shard_map/psum | solution.py:80
  1073.1 22.6 copy-start.4
  1113.7 299.4 %copy-start.33 = (f32[2048]{0:T(1024)S(1)}, f32[2048]{0:T(1024)}, u32[]{:S(2)}) copy-start(f32[2048]{0:T(1024)} %copy-done.32) | copy-start | bytes 24580
  1113.7 776.5 %all-reduce.17.cloned.1.call-start = ((), (), s32[]{:S(2)}) async-start(), calls=%async_computation.4 | async-start | bytes 16777216 | tf_op jit(solution)/shard_map/psum | solution.py:98
  1437.4 24.6 copy-start.30
  1437.4 24.6 copy-start.31
  1462.0 63.4 %copy-start.28 = (bf16[2048,4,32]{0,2,1:T(8,128)(2,1)S(1)}, bf16[2048,4,32]{0,2,1:T(8,128)(2,1)}, u32[]{:S(2)}) copy-start(bf16[2048,4,32]{0,2,1:T(8,128)(2,1)} %copy-done.27) | copy-start | bytes 1572868
  1462.0 63.4 %copy-start.29 = (bf16[2048,4,32]{0,2,1:T(8,128)(2,1)S(1)}, bf16[2048,4,32]{0,2,1:T(8,128)(2,1)}, u32[]{:S(2)}) copy-start(bf16[2048,4,32]{0,2,1:T(8,128)(2,1)} %get-tuple-element.59) | copy-start | bytes 1572868
  1525.4 64.2 %copy-start.22 = (f32[2048,32]{0,1:T(8,128)S(1)}, f32[2048,32]{0,1:T(8,128)}, u32[]{:S(2)}) copy-start(f32[2048,32]{0,1:T(8,128)} %copy-done.21) | copy-start | bytes 786436
  1525.4 64.2 %copy-start.24 = (f32[2048,32]{0,1:T(8,128)S(1)}, f32[2048,32]{0,1:T(8,128)}, u32[]{:S(2)}) copy-start(f32[2048,32]{0,1:T(8,128)} %get-tuple-element.67) | copy-start | bytes 786436
  1602.3 874.2 %all-reduce.19.cloned.1.call-start = ((), (), s32[]{:S(2)}) async-start(), calls=%async_computation.5 | async-start | bytes 96206848 | tf_op jit(solution)/shard_map/psum | solution.py:117
  1602.4 10.2 copy-start.57
  1602.4 30.3 %slice-start = ((s8[8388608]{0:T(1024)(128)(4,1)}), s8[4194304]{0:T(1024)(128)(4,1)S(1)}, s32[]{:S(2)}) async-start(s8[8388608]{0:T(1024)(128)(4,1)} %bitcast.125), calls=%async_computation.6 | async-start | bytes 8388608
  1612.5 10.1 copy-start.14
  1612.5 10.1 copy-start.55
  1612.5 20.1 slice-start.1
  1612.5 22.6 slice-start.2
  1622.6 10.1 copy-start.6
  1622.6 12.5 slice-start.3
  1635.1 255.1 %copy-start.35 = (pred[2048]{0:T(1024)(128)(4,1)S(1)}, pred[2048]{0:T(1024)(128)(4,1)}, u32[]{:S(2)}) copy-start(pred[2048]{0:T(1024)(128)(4,1)} %copy-done.34) | copy-start | bytes 6148
  2476.5 23.2 copy-start.18
  2476.5 24.8 copy-start.23
  (36 other events, 146.1 us)
Sparse Core Ops, SparseCore 0:
  32.7 291.4 all-reduce.8
  425.7 287.7 all-reduce.10
  768.2 287.7 all-reduce.12
  1113.8 287.7 all-reduce.14
  1602.4 287.7 all-reduce.16
  1923.9 552.5 all-reduce.18
where the time goes:
time: 2530 us; the launch traced here: 2520 us
  waiting for transfers between devices  1920 us (76%)
  matrix products  352 us (14%)
  other arithmetic  141 us (6%)
  local copies, waits for them, and re-layouts  67.3 us (3%)
    psum x1, waiting for transfers between devices, device_step(): return lax.psum((d_table,) + grads, 'dp')  519 us
    psum x1, waiting for transfers between devices, local_layer(): d_hidden = ALPHA * d_resid_two + lax.psum(d_hidden_part, 'tp')  288 us
    psum x1, waiting for transfers between devices, local_layer(): attn_out = lax.psum(attn_part, 'tp') + b_out.astype(jnp.float32)  288 us
    psum x1, waiting for transfers between devices, local_layer(): ffn_out = lax.psum(ffn_part, 'tp') + b_down.astype(jnp.float32)  287 us
    psum x1, waiting for transfers between devices, device_step(): embedded = lax.psum(own_rows.astype(jnp.float32), 'tp')  286 us
    psum x1, waiting for transfers between devices, local_layer(): d_embedded = ALPHA * d_resid_one + lax.psum(d_emb_part, 'tp')  250 us
    dot_general x1, matrix products, local_layer(): jnp.einsum('bhqk,bqhd->bkhd', d_scores, queries, preferred_element_type=j...  64.2 us
    dot_general x1, matrix products, local_layer(): jnp.einsum('bhqk,bkhd->bqhd', d_scores, keys_rot, preferred_element_type=...  63.4 us
  transfers between devices with their start and end apart: 6, of which 6 were waited for; matrix products, arithmetic and copies ran while one was open for 2% of the time, Pallas kernels for 0%

commit v1 on v0

v1 whole, which is shorter than its diff:
```python
import jax
import jax.numpy as jnp
from jax import lax
from jax.sharding import PartitionSpec as P

ALPHA = 140.0 ** 0.5
EPS = 1e-5
SHRINK = 0.1
ROPE_BASE = 10000.0
WEIGHT_SPECS = (P(None, 'tp'), P('tp', None), P('tp', None), P(), P(), P(), P(None, 'tp'), P('tp'), P(None, 'tp'), P('tp'), P('tp', None), P(), P())
ALL = ('tp', 'dp')
BF = jnp.bfloat16
F32 = jnp.float32


def norm_scaled(values, gain):
    mean_val = jnp.mean(values, axis=-1, keepdims=True)
    centered = values - mean_val
    variance = jnp.mean(centered * centered, axis=-1, keepdims=True)
    return centered * lax.rsqrt(variance + EPS) * gain


def geglu(gate_pre, lin_pre):
    return jax.nn.gelu(gate_pre, approximate=False) * lin_pre


def rope_tables(seq_len, head_dim):
    half_dim = head_dim // 2
    inv_freq = ROPE_BASE ** (-2.0 * jnp.arange(half_dim, dtype=F32) / head_dim)
    angles = jnp.arange(seq_len, dtype=F32)[:, None] * inv_freq[None, :]
    return jnp.cos(angles)[:, None, :], jnp.sin(angles)[:, None, :]


def apply_rope(values, cos_tab, sin_tab):
    half_dim = values.shape[-1] // 2
    first_half = values[..., :half_dim]
    second_half = values[..., half_dim:]
    return jnp.concatenate([first_half * cos_tab - second_half * sin_tab, second_half * cos_tab + first_half * sin_tab], axis=-1)


def solution(mesh):
    n_tp, n_dp = mesh.shape['tp'], mesh.shape['dp']
    in_specs = (P('dp', None), P('dp', None, None), P('tp', None)) + WEIGHT_SPECS
    out_specs = (P('tp', None),) + WEIGHT_SPECS

    def device_step(tokens, cotangent, emb_table, *weights):
        (w_qkv, b_qkv, w_out, b_out, ln1_gain, ln1_bias, w_gate, b_gate, w_lin, b_lin, w_down, b_down, ln2_gain) = weights
        tp, dp = lax.axis_index('tp'), lax.axis_index('dp')
        tokens = tokens[0]
        seq_len, width = tokens.shape[0], emb_table.shape[1]
        heads, head_dim = b_qkv.shape[0], b_qkv.shape[1] // 3
        own = seq_len // n_tp
        ffn = w_gate.shape[1]
        zero = jnp.minimum(tokens[0], 0).astype(F32)

        def rounded(values):
            return (values + zero).astype(BF)

        def gathered(weight):
            rows = weight.shape[0] // n_dp
            piece = lax.dynamic_slice_in_dim(weight, dp * rows, rows, 0).astype(F32)
            return lax.all_gather(piece, ALL, axis=0, tiled=True)

        wo_rows = w_out.shape[0] // n_dp
        wo_piece = lax.dynamic_slice_in_dim(w_out, dp * wo_rows, wo_rows, 0)
        bias_rows = jnp.concatenate([b_gate[None], b_lin[None], jnp.zeros((6, ffn), BF)], axis=0)
        wo_all = lax.all_gather(jnp.concatenate([wo_piece, bias_rows], axis=0).astype(F32), ALL, axis=0, tiled=True).reshape(n_tp, n_dp, wo_rows + 8, width)
        wo_full = rounded(wo_all[:, :, :wo_rows].reshape(n_tp, n_dp * wo_rows, width))
        bg_full, bl_full = wo_all[:, 0, wo_rows], wo_all[:, 0, wo_rows + 1]
        wg_full = rounded(gathered(w_gate).reshape(n_tp, width, ffn))
        wl_full = rounded(gathered(w_lin).reshape(n_tp, width, ffn))
        wd_full = rounded(gathered(w_down).reshape(n_tp, ffn, width))

        vocab_loc = emb_table.shape[0]
        local_ids = tokens - tp * vocab_loc
        in_shard = (local_ids >= 0) & (local_ids < vocab_loc)
        safe_ids = jnp.where(in_shard, local_ids, 0)
        own_rows = jnp.where(in_shard[:, None], jnp.take(emb_table, safe_ids, axis=0), 0.0)
        embedded = lax.psum(own_rows.astype(F32), 'tp')

        emb_bf = embedded.astype(BF)
        qkv_pre = jnp.dot(emb_bf, w_qkv, preferred_element_type=F32) + b_qkv.reshape(-1).astype(F32)
        qkv_all = qkv_pre.astype(BF).reshape(seq_len, heads, 3, head_dim)
        cos_tab, sin_tab = rope_tables(seq_len, head_dim)
        queries = apply_rope(qkv_all[:, :, 0].astype(F32), cos_tab, sin_tab).astype(BF)
        keys_rot = apply_rope(qkv_all[:, :, 1].astype(F32), cos_tab, sin_tab).astype(BF)
        values = qkv_all[:, :, 2]
        attn_scale = head_dim ** -0.5
        causal = jnp.arange(seq_len)[:, None] >= jnp.arange(seq_len)[None, :]
        scores = jnp.einsum('qhd,khd->hqk', queries, keys_rot, preferred_element_type=F32) * attn_scale
        attn_probs = jax.nn.softmax(jnp.where(causal, scores, -1e30), axis=-1).astype(BF)
        context = jnp.einsum('hqk,khd->qhd', attn_probs, values, preferred_element_type=F32).reshape(n_tp, own, heads * head_dim)
        ctx_own = (lax.all_to_all(context, 'tp', 0, 0) + zero).astype(BF)

        emb_own = lax.dynamic_slice_in_dim(embedded, tp * own, own, 0)
        cot_own = lax.dynamic_slice_in_dim(cotangent[0], tp * own, own, 0).astype(F32)
        attn_out = jnp.einsum('hse,hed->sd', ctx_own, wo_full, preferred_element_type=F32) + b_out.astype(F32)
        normed_one, norm_one_pull = jax.vjp(norm_scaled, ALPHA * emb_own + attn_out, ln1_gain.astype(F32))
        hidden = (normed_one + ln1_bias.astype(F32)).astype(BF)
        gate_pre = jnp.einsum('sk,tkc->tsc', hidden, wg_full, preferred_element_type=F32) + bg_full[:, None]
        lin_pre = jnp.einsum('sk,tkc->tsc', hidden, wl_full, preferred_element_type=F32) + bl_full[:, None]
        inner_val, act_pull = jax.vjp(geglu, gate_pre, lin_pre)
        inner_act = inner_val.astype(BF)
        ffn_out = jnp.einsum('tsc,tcd->sd', inner_act, wd_full, preferred_element_type=F32) + b_down.astype(F32)
        norm_two_pull = jax.vjp(norm_scaled, ALPHA * hidden.astype(F32) + ffn_out, ln2_gain.astype(F32))[1]

        d_resid_two, d_ln2_gain = norm_two_pull(cot_own)
        d_b_down = jnp.sum(d_resid_two, axis=0)
        d_ffn_bf = d_resid_two.astype(BF)
        d_w_down = jnp.einsum('tsc,sd->tcd', inner_act, d_ffn_bf, preferred_element_type=F32)
        d_inner = jnp.einsum('sd,tcd->tsc', d_ffn_bf, wd_full, preferred_element_type=F32).astype(BF)
        d_gate_pre, d_lin_pre = act_pull(d_inner.astype(F32))
        d_b_gate = jnp.sum(d_gate_pre, axis=1)
        d_b_lin = jnp.sum(d_lin_pre, axis=1)
        d_gate_bf = d_gate_pre.astype(BF)
        d_lin_bf = d_lin_pre.astype(BF)
        d_w_gate = jnp.einsum('sk,tsc->tkc', hidden, d_gate_bf, preferred_element_type=F32)
        d_w_lin = jnp.einsum('sk,tsc->tkc', hidden, d_lin_bf, preferred_element_type=F32)
        d_hidden = ALPHA * d_resid_two + jnp.einsum('tsc,tkc->sk', d_gate_bf, wg_full, preferred_element_type=F32) + jnp.einsum('tsc,tkc->sk', d_lin_bf, wl_full, preferred_element_type=F32)
        d_ln1_bias = jnp.sum(d_hidden, axis=0)
        d_resid_one, d_ln1_gain = norm_one_pull(d_hidden)
        d_b_out = jnp.sum(d_resid_one, axis=0)
        d_attn_bf = d_resid_one.astype(BF)
        d_w_out = jnp.einsum('hse,sd->hed', ctx_own, d_attn_bf, preferred_element_type=F32)
        d_ctx = jnp.einsum('sd,hed->hse', d_attn_bf, wo_full, preferred_element_type=F32)
        d_context = (lax.all_to_all(d_ctx, 'tp', 0, 0) + zero).astype(BF).reshape(seq_len, heads, head_dim)

        def reduced(grad):
            piece = lax.psum_scatter(grad.reshape(-1, grad.shape[-1]), ALL, scatter_dimension=0, tiled=True)
            return lax.all_gather(piece, 'dp', axis=0, tiled=True)

        d_w_down, d_w_gate, d_w_lin, d_w_out = reduced(d_w_down), reduced(d_w_gate), reduced(d_w_lin), reduced(d_w_out)

        d_probs = jnp.einsum('qhd,khd->hqk', d_context, values, preferred_element_type=F32)
        d_values = jnp.einsum('hqk,qhd->khd', attn_probs, d_context, preferred_element_type=F32)
        probs_f32 = attn_probs.astype(F32)
        d_scores = (probs_f32 * (d_probs - jnp.sum(d_probs * probs_f32, axis=-1, keepdims=True)) * attn_scale).astype(BF)
        d_queries = apply_rope(jnp.einsum('hqk,khd->qhd', d_scores, keys_rot, preferred_element_type=F32), cos_tab, -sin_tab)
        d_keys = apply_rope(jnp.einsum('hqk,qhd->khd', d_scores, queries, preferred_element_type=F32), cos_tab, -sin_tab)
        d_qkv = jnp.stack([d_queries, d_keys, d_values], axis=2).reshape(seq_len, -1)
        d_b_qkv = jnp.sum(d_qkv, axis=0)
        d_qkv_bf = d_qkv.astype(BF)
        d_w_qkv = jnp.dot(emb_bf.T, d_qkv_bf, preferred_element_type=F32)
        d_emb_part = jnp.dot(d_qkv_bf, w_qkv.T, preferred_element_type=F32)
        d_emb_part = lax.dynamic_update_slice_in_dim(d_emb_part, lax.dynamic_slice_in_dim(d_emb_part, tp * own, own, 0) + ALPHA * d_resid_one, tp * own, 0)
        d_embedded = lax.psum(d_emb_part, 'tp')
        d_rows = jnp.where(in_shard[:, None], SHRINK * d_embedded, 0.0)
        d_table = jax.ops.segment_sum(d_rows, safe_ids, num_segments=vocab_loc)

        slot = (jnp.arange(n_tp) == tp).astype(F32)[:, None]
        d_bq_rows = jnp.pad(slot * d_b_qkv[None], ((0, 0), (0, width - d_b_qkv.shape[0])))
        small = jnp.concatenate([d_b_gate, d_b_lin, d_bq_rows, jnp.stack([d_b_out, d_ln1_gain, d_ln1_bias, d_b_down, d_ln2_gain])], axis=0)
        small = lax.psum(small, ALL)
        d_b_gate = lax.dynamic_index_in_dim(small[:n_tp], tp, 0, keepdims=False)
        d_b_lin = lax.dynamic_index_in_dim(small[n_tp:2 * n_tp], tp, 0, keepdims=False)
        d_b_qkv = lax.dynamic_index_in_dim(small[2 * n_tp:3 * n_tp], tp, 0, keepdims=False)[:d_b_qkv.shape[0]].reshape(heads, 3 * head_dim)
        d_b_out, d_ln1_gain, d_ln1_bias, d_b_down, d_ln2_gain = [small[3 * n_tp + i] for i in range(5)]
        d_table, d_w_qkv = lax.psum((d_table, d_w_qkv), 'dp')
        return (d_table, d_w_qkv, d_b_qkv, d_w_out, d_b_out, d_ln1_gain, d_ln1_bias, d_w_gate, d_b_gate, d_w_lin, d_b_lin, d_w_down, d_b_down, d_ln2_gain)

    return jax.shard_map(device_step, mesh=mesh, in_specs=in_specs, out_specs=out_specs, check_vma=False)
```

time: 2530 us -> 2260 us (0.89)
  waiting for transfers between devices: 1920 us -> 1570 us
  blocking collectives: 24.9 us -> 60.1 us
  matrix products: 352 us -> 383 us
    psum x6 -> x4, waiting for transfers between devices: 1920 us -> 717 us  [the longest x1 406 us: device_step(): d_table, d_w_qkv = lax.psum((d_table, d_w_qkv), 'dp')]
    reduce_scatter x0 -> x4, waiting for transfers between devices: none -> 654 us  [reduced(): lax.psum_scatter(grad.reshape(-1, grad.shape[-1]), ALL, scatter_dimension...]
    all_gather x0 -> x8, waiting for transfers between devices: none -> 140 us  [the longest x3 140 us: gathered(): return lax.all_gather(piece, ALL, axis=0, tiled=True)]
    all_to_all x0 -> x1, waiting for transfers between devices: none -> 63.3 us  [device_step(): ctx_own = (lax.all_to_all(context, 'tp', 0, 0) + zero).astype(BF)]
    all_to_all x0 -> x1, blocking collectives: none -> 60.1 us  [device_step(): lax.all_to_all(d_ctx, 'tp', 0, 0) + zero]
    convert_element_type x12 -> x19, other arithmetic: 41.3 us -> 76 us  [the longest x1 33.3 us: device_step(): jax.nn.softmax(jnp.where(causal, scores, -1e+30), axis=-1).astype(BF)]
    dot_general x20, matrix products: 318 us -> 348 us  [the longest x1 64.3 us: device_step(): jnp.einsum('hqk,qhd->khd', d_scores, queries, preferred_element_type=F32)]
  transfers between devices with their start and end apart: 6 -> 17, of which waited for: 6 -> 8; matrix products, arithmetic and copies ran while one was open for 2% -> 19% of each run, Pallas kernels for 0% -> 0%
where the time goes in v1:
time: 2260 us
  waiting for transfers between devices  1570 us (69%)
  matrix products  383 us (17%)
  other arithmetic  136 us (6%)
  local copies, waits for them, and re-layouts  82.1 us (4%)
  blocking collectives  60.1 us (3%)
    reduce_scatter x4, waiting for transfers between devices, reduced(): lax.psum_scatter(grad.reshape(-1, grad.shape[-1]), ALL, scatter_dimension...  654 us
    psum x1, waiting for transfers between devices, device_step(): d_table, d_w_qkv = lax.psum((d_table, d_w_qkv), 'dp')  406 us
    psum x1, waiting for transfers between devices, device_step(): embedded = lax.psum(own_rows.astype(F32), 'tp')  311 us
    all_gather x3, waiting for transfers between devices, gathered(): return lax.all_gather(piece, ALL, axis=0, tiled=True)  140 us
    dot_general x1, matrix products, device_step(): jnp.einsum('hqk,qhd->khd', d_scores, queries, preferred_element_type=F32)  64.3 us
    dot_general x1, matrix products, device_step(): jnp.einsum('hqk,khd->qhd', d_scores, keys_rot, preferred_element_type=F32)  63.4 us
    all_to_all x1, waiting for transfers between devices, device_step(): ctx_own = (lax.all_to_all(context, 'tp', 0, 0) + zero).astype(BF)  63.3 us
    all_to_all x1, blocking collectives, device_step(): lax.all_to_all(d_ctx, 'tp', 0, 0) + zero  60.1 us
  transfers between devices with their start and end apart: 17, of which 8 were waited for; matrix products, arithmetic and copies ran while one was open for 19% of the time, Pallas kernels for 0%

profile of v1, /device:TPU:0, one launch (start us, length us, event | category | flops | bytes accessed | tf_op | source)
XLA Modules:
  0.0 2257.8 jit_solution(11339095616495640469)
XLA Ops:
  9.5 18.4 gather_fusion
  27.9 5.5 select_convert_fusion
  47.7 310.9 %all-reduce.7.cloned.1.call-done = f32[2048,1024]{1,0:T(8,128)} async-done(((f32[2048,1024]{1,0:T(8,128)}), f32[2048,1024]{1,0:T(8,128)}) %all-reduce.7.cloned.1.call-update) | async-done | bytes 8388624 | tf_op jit(solution)/shard_map/psum | solution.py:79
  358.6 7.1 add_convert_fusion.3
  367.9 34.1 %fusion.106 = (f32[4,2048]{1,0:T(4,128)S(1)}, f32[4,2048,2048]{1,2,0:T(8,128)}) fusion(pred[2048,2048]{0,1:T(8,128)(4,1)} %iota_compare_fusion, bf16[2048,4,32]{0,2,1:T(8,128)(2,1)} %get-tuple-element.50, bf16[2048,4,32]{0,2,1:T(8,128)(2,1)} %get-tuple-element.51, bf16[2048,4,32]{0,2,1:T(8,128)(2,1)S(1)} %get-tuple-element.43, ...), kind=kOutput, calls=%fused_computation.189 | convolution fusion | flops 2218788864 | bytes 73433088 | tf_op jit(solution)/shard_map/sub | solution.py:91
  402.1 33.3 %divide_convert_fusion = bf16[4,2048,2048]{1,2,0:T(8,128)(2,1)} fusion(f32[4,2048,2048]{1,2,0:T(8,128)} %get-tuple-element.66, f32[4,2048]{1,0:T(4,128)S(1)} %get-tuple-element.65), kind=kLoop, calls=%fused_computation.8 | loop fusion | flops 33554432 | bytes 100696064 | tf_op jit(solution)/shard_map/convert_element_type | solution.py:91
  435.3 18.1 convolution_bitcast_fusion.1
  471.6 63.3 %all-to-all-done = f32[4,512,256]{2,1,0:T(8,128)} async-done(((f32[4,512,256]{2,1,0:T(8,128)}), f32[4,512,256]{2,1,0:T(8,128)}, u32[]{:S(2)}, u32[]{:S(2)}) %all-to-all-start) | async-done | bytes 2097184 | tf_op jit(solution)/shard_map/all_to_all | solution.py:93
  540.9 48.9 %all-gather.15.cloned.1.call-done = f32[4096,1024]{1,0:T(8,128)} async-done(((f32[128,1024]{1,0:T(8,128)}), f32[4096,1024]{1,0:T(8,128)}) %all-gather.15.cloned.1.call-update) | async-done | bytes 16777232 | tf_op jit(solution)/shard_map/all_gather | solution.py:62
  589.8 15.1 add_convert_fusion
  608.1 6.8 fusion.67
  614.9 90.8 %all-gather.13.cloned.1.call-done = f32[4096,1024]{1,0:T(8,128)} async-done(((f32[128,1024]{1,0:T(8,128)}), f32[4096,1024]{1,0:T(8,128)}) %all-gather.13.cloned.1.call-update) | async-done | bytes 16777232 | tf_op jit(solution)/shard_map/all_gather | solution.py:62
  705.7 7.2 add_convert_fusion.1
  713.0 27.3 %fusion.14 = (bf16[4,512,1024]{2,1,0:T(8,128)(2,1)S(1)}, f32[4,512,1024]{2,1,0:T(8,128)}, f32[4,512,1024]{2,1,0:T(8,128)}, f32[4,1024,512]{1,2,0:T(8,128)}) fusion(f32[4,1024]{1,0:T(4,128)S(1)} %get-tuple-element.76, f32[4,1024,512]{1,2,0:T(8,128)} %fusion.67, f32[4,1024]{1,0:T(4,128)S(1)} %get-tuple-element.77, bf16[4,1024,1024]{2,1,0:T(8,128)(2,1)S(1)} %bitcast.250, ...), kind=kOutput, calls=%fused_computation.29 | convolution fusion | flops 4437573632 | bytes 47218688 | tf_op jit(solution)/shard_map/sk,tkc->tsc/dot_general | solution.py:101
  749.0 22.4 fusion.98
  771.5 10.6 fusion.55
  782.1 15.3 multiply_reduce_fusion
  806.4 13.2 fusion.78
  819.7 15.4 fusion.64
  835.2 12.9 fusion.53
  851.7 60.1 %all_to_all.10 = f32[4,512,256]{2,1,0:T(8,128)S(1)} all-to-all(f32[4,512,256]{2,1,0:T(8,128)S(1)} %convolution_bitcast_fusion.2), channel_id=1, replica_groups=mesh['tp'=4,'dp'=8] {'tp'}, dimensions={0} | all-to-all | bytes 4194304 | tf_op jit(solution)/shard_map/all_to_all | solution.py:126
  915.6 24.5 %fusion.71 = f32[4,2048,2048]{1,2,0:T(8,128)} fusion(bf16[2048,4,64]{0,2,1:T(8,128)(2,1)S(1)} %reshape.278, bf16[2048,4,3,64]{0,3,2,1:T(8,128)(2,1)} %bitcast.242), kind=kOutput, calls=%fused_computation.135 | convolution fusion | flops 2147483648 | bytes 69206016 | tf_op jit(solution)/shard_map/qhd,khd->hqk/dot_general | solution.py:134
  940.1 64.3 %fusion.46 = f32[2048,4,64]{0,2,1:T(8,128)} fusion(bf16[4,2048,2048]{1,2,0:T(8,128)(2,1)} %divide_convert_fusion, f32[4,2048,2048]{1,2,0:T(8,128)} %fusion.71, bf16[2048,4,32]{0,2,1:T(8,128)(2,1)S(1)} %copy-done.22, bf16[2048,4,32]{0,2,1:T(8,128)(2,1)} %get-tuple-element.51), kind=kOutput, calls=%fused_computation.73 | convolution fusion | flops 2267031552 | bytes 103809024 | tf_op jit(solution)/shard_map/hqk,qhd->khd/dot_general | solution.py:139
  1004.4 63.4 %fusion.45 = f32[2048,4,64]{0,2,1:T(8,128)} fusion(bf16[4,2048,2048]{1,2,0:T(8,128)(2,1)} %divide_convert_fusion, f32[4,2048,2048]{1,2,0:T(8,128)} %fusion.71, bf16[2048,4,32]{0,2,1:T(8,128)(2,1)} %copy-done.21, bf16[2048,4,32]{0,2,1:T(8,128)(2,1)} %copy-done.20), kind=kOutput, calls=%fused_computation.72 | convolution fusion | flops 2267031552 | bytes 103809024 | tf_op jit(solution)/shard_map/hqk,khd->qhd/dot_general | solution.py:138
  1073.9 16.5 convolution_bitcast_fusion
  1109.7 105.9 %reduce-scatter.11.cloned.1.call-done = f32[128,1024]{1,0:T(8,128)} async-done(((f32[4096,1024]{1,0:T(8,128)}), f32[128,1024]{1,0:T(8,128)}) %reduce-scatter.11.cloned.1.call-update) | async-done | bytes 524304 | tf_op jit(solution)/shard_map/reduce_scatter | solution.py:129
  1215.7 320.4 %reduce-scatter.9.cloned.1.call-done = f32[128,1024]{1,0:T(8,128)} async-done(((f32[4096,1024]{1,0:T(8,128)}), f32[128,1024]{1,0:T(8,128)}) %reduce-scatter.9.cloned.1.call-update) | async-done | bytes 524304 | tf_op jit(solution)/shard_map/reduce_scatter | solution.py:129
  1536.2 227.2 %reduce-scatter.7.cloned.1.call-done = f32[128,1024]{1,0:T(8,128)} async-done(((f32[4096,1024]{1,0:T(8,128)}), f32[128,1024]{1,0:T(8,128)}) %reduce-scatter.7.cloned.1.call-update) | async-done | bytes 524304 | tf_op jit(solution)/shard_map/reduce_scatter | solution.py:129
  1763.5 9.4 fusion.57
  1772.9 32.3 %scatter_custom_fusion = f32[7648,1024]{1,0:T(8,128)} fusion(s32[2048]{0:T(1024)} %bitcast.263, f32[]{:T(128)} %constant.56.clone.1, f32[2048,1024]{1,0:T(8,128)} %all-reduce.9.cloned.1.call-done, f32[]{:T(128)} %constant.150.clone.1, pred[2048]{0:T(1024)(128)(4,1)S(1)} %copy-done.24), kind=kCustom, calls=%fused_computation.22 | custom fusion | flops 6291456 | bytes 39718400 | tf_op jit(solution)/shard_map/scatter-add | solution.py:148
  1809.6 406.4 %all-reduce.13.cloned.1.call-done = (f32[7648,1024]{1,0:T(8,128)}, f32[1024,768]{1,0:T(8,128)}) async-done(((f32[7648,1024]{1,0:T(8,128)}, f32[1024,768]{1,0:T(8,128)}), (f32[7648,1024]{1,0:T(8,128)}, f32[1024,768]{1,0:T(8,128)})) %all-reduce.13.cloned.1.call-update) | async-done | bytes 34471952 | tf_op jit(solution)/shard_map/psum | solution.py:158
  2216.1 22.4 copy.104
  (199 shorter events, 111.1 us)
Async XLA Ops:
  8.0 350.6 %copy-start = (bf16[1024,768]{1,0:T(8,128)(2,1)S(1)}, bf16[1024,768]{1,0:T(8,128)(2,1)}, u32[]{:S(2)}) copy-start(bf16[1024,768]{1,0:T(8,128)(2,1)} %param.19) | copy-start | bytes 4718596
  8.0 350.6 %all-reduce.7.cloned.1.call-start = ((), (), s32[]{:S(2)}) async-start(), calls=%async_computation.6 | async-start | bytes 16777216 | tf_op jit(solution)/shard_map/psum | solution.py:79
  9.5 18.4 copy-start.23
  33.4 433.1 %all-gather.9.cloned.1.call-start = ((), (), s32[]{:S(2)}) async-start(), calls=%async_computation.7 | async-start | bytes 5406720 | tf_op jit(solution)/shard_map/all_gather | solution.py:67
  35.8 505.1 %all-gather.11.cloned.1.call-start = ((), (), s32[]{:S(2)}) async-start(), calls=%async_computation.8 | async-start | bytes 17301504 | tf_op jit(solution)/shard_map/all_gather | solution.py:62
  37.7 552.1 %all-gather.15.cloned.1.call-start = ((), (), s32[]{:S(2)}) async-start(), calls=%async_computation.10 | async-start | bytes 17301504 | tf_op jit(solution)/shard_map/all_gather | solution.py:62
  39.6 666.2 %all-gather.13.cloned.1.call-start = ((), (), s32[]{:S(2)}) async-start(), calls=%async_computation.9 | async-start | bytes 17301504 | tf_op jit(solution)/shard_map/all_gather | solution.py:62
  43.6 322.7 %copy-start.15 = (f32[2048,32]{0,1:T(8,128)}, f32[2048,32]{0,1:T(8,128)S(1)}, u32[]{:S(2)}) copy-start(f32[2048,32]{0,1:T(8,128)S(1)} %get-tuple-element.64) | copy-start | bytes 786436
  367.9 34.1 %copy-start.20 = (bf16[2048,4,32]{0,2,1:T(8,128)(2,1)}, bf16[2048,4,32]{0,2,1:T(8,128)(2,1)S(1)}, u32[]{:S(2)}) copy-start(bf16[2048,4,32]{0,2,1:T(8,128)(2,1)S(1)} %get-tuple-element.42) | copy-start | bytes 1572868
  367.9 34.1 %copy-start.21 = (bf16[2048,4,32]{0,2,1:T(8,128)(2,1)}, bf16[2048,4,32]{0,2,1:T(8,128)(2,1)S(1)}, u32[]{:S(2)}) copy-start(bf16[2048,4,32]{0,2,1:T(8,128)(2,1)S(1)} %get-tuple-element.43) | copy-start | bytes 1572868
  457.1 9.4 copy-start.37
  460.0 74.9 %all-to-all-start = ((f32[4,512,256]{2,1,0:T(8,128)}), f32[4,512,256]{2,1,0:T(8,128)}, u32[]{:S(2)}, u32[]{:S(2)}) async-start(f32[4,512,256]{2,1,0:T(8,128)} %copy.64), calls=%async_computation | async-start | bytes 4194304 | tf_op jit(solution)/shard_map/all_to_all | solution.py:93
  464.5 644.7 %reduce-scatter.5.cloned.1.call-start = ((), (), s32[]{:S(2)}) async-start(), calls=%async_computation.13 | async-start | bytes 4325376 | tf_op jit(solution)/shard_map/reduce_scatter | solution.py:129
  705.7 34.6 %slice-start = ((s8[8388608]{0:T(1024)(128)(4,1)}), s8[4194304]{0:T(1024)(128)(4,1)S(1)}, s32[]{:S(2)}) async-start(s8[8388608]{0:T(1024)(128)(4,1)} %bitcast.247), calls=%async_computation.22 | async-start | bytes 8388608
  713.0 27.4 %copy-start.9 = (bf16[4096,1024]{1,0:T(8,128)(2,1)}, bf16[4096,1024]{1,0:T(8,128)(2,1)S(1)}, u32[]{:S(2)}) copy-start(bf16[4096,1024]{1,0:T(8,128)(2,1)S(1)} %add_convert_fusion.1) | copy-start | bytes 25165828
  713.0 27.4 %slice-start.1 = ((s8[8388608]{0:T(1024)(128)(4,1)}), s8[4194304]{0:T(1024)(128)(4,1)S(1)}, s32[]{:S(2)}) async-start(s8[8388608]{0:T(1024)(128)(4,1)} %bitcast.247), calls=%async_computation.23 | async-start | bytes 8388608
  771.5 10.7 copy-start.4
  806.2 409.5 %reduce-scatter.11.cloned.1.call-start = ((), (), s32[]{:S(2)}) async-start(), calls=%async_computation.19 | async-start | bytes 17301504 | tf_op jit(solution)/shard_map/reduce_scatter | solution.py:129
  819.7 716.4 %reduce-scatter.9.cloned.1.call-start = ((), (), s32[]{:S(2)}) async-start(), calls=%async_computation.17 | async-start | bytes 17301504 | tf_op jit(solution)/shard_map/reduce_scatter | solution.py:129
  835.2 928.2 %reduce-scatter.7.cloned.1.call-start = ((), (), s32[]{:S(2)}) async-start(), calls=%async_computation.15 | async-start | bytes 17301504 | tf_op jit(solution)/shard_map/reduce_scatter | solution.py:129
  848.1 924.8 %all-reduce.9.cloned.1.call-start = ((), (), s32[]{:S(2)}) async-start(), calls=%async_computation.11 | async-start | bytes 16777216 | tf_op jit(solution)/shard_map/psum | solution.py:146
  915.6 24.6 %copy-start.22 = (bf16[2048,4,32]{0,2,1:T(8,128)(2,1)S(1)}, bf16[2048,4,32]{0,2,1:T(8,128)(2,1)}, u32[]{:S(2)}) copy-start(bf16[2048,4,32]{0,2,1:T(8,128)(2,1)} %get-tuple-element.50) | copy-start | bytes 1572868
  1004.4 63.4 %copy-start.16 = (f32[2048,32]{0,1:T(8,128)S(1)}, f32[2048,32]{0,1:T(8,128)}, u32[]{:S(2)}) copy-start(f32[2048,32]{0,1:T(8,128)} %copy-done.15) | copy-start | bytes 786436
  1004.4 63.4 %copy-start.18 = (f32[2048,32]{0,1:T(8,128)S(1)}, f32[2048,32]{0,1:T(8,128)}, u32[]{:S(2)}) copy-start(f32[2048,32]{0,1:T(8,128)} %get-tuple-element.62) | copy-start | bytes 786436
  1101.9 703.4 %all-reduce.11.cloned.1.call-start = ((), (), s32[]{:S(2)}) async-start(), calls=%async_computation.12 | async-start | bytes 196608 | tf_op jit(solution)/shard_map/psum | solution.py:153
  1109.1 700.4 %all-gather.17.cloned.1.call-start = ((), (), s32[]{:S(2)}) async-start(), calls=%async_computation.14 | async-start | bytes 1179648 | tf_op jit(solution)/shard_map/all_gather | solution.py:130
  1109.7 699.9 %all-gather.23.cloned.1.call-start = ((), (), s32[]{:S(2)}) async-start(), calls=%async_computation.20 | async-start | bytes 4718592 | tf_op jit(solution)/shard_map/all_gather | solution.py:130
  1215.7 593.9 %all-gather.21.cloned.1.call-start = ((), (), s32[]{:S(2)}) async-start(), calls=%async_computation.18 | async-start | bytes 4718592 | tf_op jit(solution)/shard_map/all_gather | solution.py:130
  1536.1 273.5 %all-gather.19.cloned.1.call-start = ((), (), s32[]{:S(2)}) async-start(), calls=%async_computation.16 | async-start | bytes 4718592 | tf_op jit(solution)/shard_map/all_gather | solution.py:130
  1763.4 9.5 copy-start.24
  1763.4 452.6 %all-reduce.13.cloned.1.call-start = ((), (), s32[]{:S(2)}) async-start(), calls=%async_computation.21 | async-start | bytes 68943872 | tf_op jit(solution)/shard_map/psum | solution.py:158
  2216.1 22.4 copy-start.14
  (25 other events, 115.8 us)
Sparse Core Ops, SparseCore 0:
  33.5 325.0 all-reduce.6
  1101.9 314.2 all-reduce.8
  1422.4 157.0 all-reduce.10
  1581.3 33.2 all-gather.16
  1616.3 49.2 all-gather.22
  1667.3 46.1 all-gather.20
  1763.5 38.0 all-gather.18
  1806.8 409.2 all-reduce.12
Sparse Core Ops, SparseCore 1:
  37.4 224.4 all-gather.8
  264.6 177.3 all-gather.10
  444.7 145.1 all-gather.14
  593.3 112.4 all-gather.12
  806.3 144.1 reduce-scatter.4
  952.7 262.9 reduce-scatter.10
  1217.8 318.2 reduce-scatter.8
  1538.9 224.5 reduce-scatter.6
